TPU v7x, 32 devices: a whole 2x2x4 slice. The times are simulated.
32 devices in a mesh: grp: 2 (over y), slab: 4 (over z), row: 2 (over x), col: 2 (over core).
Axes of the slice: x: 2, y: 2, z: 4, core: 2. Of those that a mesh axis runs over, the one named last changes fastest.
Arguments:
- image: float32 [3, 64, 32, 256], P(None, ('grp', 'slab'), 'row', 'col'), parts along dimension 1, may hold values from -28 to 28, as said below
- brain_mask: int32 [64, 32, 256], P(('grp', 'slab'), 'row', 'col'), parts along dimension 0, may hold values from 0 to 1, as said below
- labels: int32 [64, 32, 256], P(('grp', 'slab'), 'row', 'col'), parts along dimension 0, may hold values from 0 to 7
Outputs:
- posterior: bfloat16 [8, 64, 32, 256], P(None, ('grp', 'slab'), 'row', 'col'), parts along dimension 1
- bias_field: float32 [3, 64, 32, 256], P(None, ('grp', 'slab'), 'row', 'col'), parts along dimension 1
- class_means: float32 [16, 3], P('grp'), parts along dimension 0
There are 2 independent parts, one for each index of `grp`. A program takes and returns all parts, laid end to end along the dimension named above; each array names one. Nothing has to cross between parts.
Inputs may be any that keep to these rules, and one draw needn't show every extreme that they name: `image`: log intensities of 3 modalities. `brain_mask`: 1 marks a brain cell, 0 a cell outside.
All inputs are finite; a program needn't handle non-finite values.
Results may differ from a plain program's by a relative error of at most 0.001.
Values sent between devices are 32-bit elements; how exact they have to be, the bound alone decides.
No kernel may reach another device: no remote copies, remote signals or barrier semaphores. Data moves between devices by JAX's collectives and lax.ppermute only.
A program may use at most 64 MiB of HBM per device.

v0:
```python
import math
import jax
import jax.numpy as jnp
from jax import lax
from jax.sharding import PartitionSpec as P

M = 3
K = 8
EM_ITERS = 2
MF_PASSES = 2
highest = lax.Precision.HIGHEST
coupling = 1.0
breadth = 8.0


def extended(cells, sides, width):
    for axis, dim in sides:
        count = lax.axis_size(axis)
        ends = count - 1
        head = lax.slice_in_dim(cells, 0, width, axis=dim)
        tail = lax.slice_in_dim(cells, cells.shape[dim] - width, cells.shape[dim], axis=dim)
        cells = jnp.concatenate(
            [
                lax.ppermute(tail, axis, [(i, (i + 1) % count) for i in range(ends)]),
                cells,
                lax.ppermute(head, axis, [((i + 1) % count, i) for i in range(ends)]),
            ],
            axis=dim,
        )
    return cells


def circulant(length):
    index = jnp.arange(length, dtype=jnp.int32)
    folded = jnp.minimum(index, length - index).astype(jnp.float32) / length
    response = jnp.exp(-2.0 * math.pi**2 * (length / breadth) ** 2 * folded * folded)
    product = index[:, None] * index[None, :] % length
    angles = 2.0 * math.pi / length * product.astype(jnp.float32)
    cosine = jnp.cos(angles)
    sine = jnp.sin(angles)
    even_part = jnp.dot(cosine * response[None, :], cosine.T, precision=highest)
    odd_part = jnp.dot(sine * response[None, :], sine.T, precision=highest)
    return (even_part + odd_part) / length


def neighbour_sum(belief):
    padded = extended(belief, (("slab", 1), ("row", 2), ("col", 3)), 1)
    total = padded[:, 2:, 1:-1, 1:-1] + padded[:, :-2, 1:-1, 1:-1]
    total = total + padded[:, 1:-1, 2:, 1:-1] + padded[:, 1:-1, :-2, 1:-1]
    total = total + padded[:, 1:-1, 1:-1, 2:] + padded[:, 1:-1, 1:-1, :-2]
    return total


def class_moments(belief, corrected):
    flat = belief.reshape(K, -1)
    values = corrected.reshape(M, -1)
    count, first, squares = lax.psum(
        (
            jnp.sum(flat, axis=1),
            jnp.dot(flat, values.T, precision=highest),
            jnp.dot(flat, (values * values).T, precision=highest),
        ),
        ("slab", "row", "col"),
    )
    means = first / (count + 1.0)[:, None]
    spread = squares - 2.0 * means * first + means * means * count[:, None]
    variance = (spread + 1.0) / (count + 1.0)[:, None]
    return (count, means, variance)


def log_density(corrected, means, variance, prior):
    offset = corrected[None] - means[:, :, None, None, None]
    terms = (
        offset * offset / variance[:, :, None, None, None]
        + jnp.log(variance)[:, :, None, None, None]
    )
    return jnp.log(prior)[:, None, None, None] - 0.5 * jnp.sum(terms, axis=1)


def smoothed(residual, column_local, row_table, slab_table):
    across = jnp.einsum(
        "msrc,cd->msrd",
        lax.all_gather(residual, "col", axis=3, tiled=True),
        column_local,
        precision=highest,
    )
    mixed = jnp.einsum(
        "msrc,rq->msqc",
        lax.all_to_all(across, "row", split_axis=1, concat_axis=2, tiled=True),
        row_table,
        precision=highest,
    )
    across = lax.all_to_all(mixed, "row", split_axis=2, concat_axis=1, tiled=True)
    mixed = jnp.einsum(
        "msrc,sq->mqrc",
        lax.all_to_all(across, "slab", split_axis=2, concat_axis=1, tiled=True),
        slab_table,
        precision=highest,
    )
    return lax.all_to_all(mixed, "slab", split_axis=1, concat_axis=2, tiled=True)


def local(image, brain_mask, labels):
    channels, slabs, rows, columns = image.shape
    inside = brain_mask.astype(jnp.float32)
    kinds = jnp.arange(K, dtype=jnp.int32)
    belief = (labels[None] == kinds[:, None, None, None]).astype(jnp.float32) * inside[None]
    column_table = circulant(columns * lax.axis_size("col"))
    column_local = lax.dynamic_slice_in_dim(
        column_table, lax.axis_index("col") * columns, columns, 1
    )
    row_table = circulant(rows * lax.axis_size("row"))
    slab_table = circulant(slabs * lax.axis_size("slab"))
    bias_field = jnp.zeros_like(image)
    means = jnp.zeros((K, channels), jnp.float32)
    for iteration in range(EM_ITERS):
        corrected = image - bias_field
        count, means, variance = class_moments(belief, corrected)
        prior = (count + 1.0) / (jnp.sum(count) + K)
        total = jnp.sum(belief, axis=0)
        removed = jnp.dot(means.T, belief.reshape(K, -1), precision=highest).reshape(image.shape)
        residual = image * total[None] - removed
        bias_field = smoothed(residual, column_local, row_table, slab_table)
        corrected = image - bias_field
        density = log_density(corrected, means, variance, prior)
        for sweep_index in range(MF_PASSES):
            belief = (
                jax.nn.softmax(density + coupling * neighbour_sum(belief), axis=0) * inside[None]
            )
    return (belief.astype(jnp.bfloat16), bias_field, means)


def solution(mesh):
    placed = (
        P(None, ("grp", "slab"), "row", "col"),
        P(("grp", "slab"), "row", "col"),
        P(("grp", "slab"), "row", "col"),
    )
    return jax.shard_map(
        local,
        mesh=mesh,
        in_specs=placed,
        out_specs=(
            P(None, ("grp", "slab"), "row", "col"),
            P(None, ("grp", "slab"), "row", "col"),
            P("grp", None),
        ),
        check_vma=False,
    )
```

profile of v0, /device:TPU:0, one launch (start us, length us, event | category | flops | bytes accessed | tf_op | source)
XLA Modules:
  0.0 240.7 jit_solution(11587355852781525625)
XLA Ops:
  6.4 35.4 %all-reduce.1 = (f32[8,3]{0,1:T(4,128)S(1)}, f32[8,3]{0,1:T(4,128)S(1)}, f32[8]{0:T(128)S(1)}) all-reduce(f32[8,3]{0,1:T(4,128)S(1)} %fusion.2, f32[8,3]{0,1:T(4,128)S(1)} %convolution_bitcast_fusion.6, f32[8]{0:T(128)S(1)} %select_reduce_fusion), channel_id=1, replica_groups=mesh['grp'=2,'slab'=4,'row'=2,'col'=2] {'slab','row','col'}, use_global_device_ids=true, to_apply=%region_5.6 | all-reduce | flops 56 | bytes 448 | tf_op jit(solution)/shard_map/psum | solution.py:57
  44.3 2.2 all_gather.6
  47.7 3.4 %all-to-all-start = ((f32[3,8,16,128]{3,2,0,1:T(8,128)}), f32[3,8,16,128]{3,2,0,1:T(8,128)S(1)}, u32[]{:S(2)}, u32[]{:S(2)}) async-start(f32[3,8,16,128]{3,2,0,1:T(8,128)} %fusion.39), calls=%async_computation | async-start | bytes 393216 | tf_op jit(solution)/shard_map/all_to_all | solution.py:89
  51.6 4.5 %all-to-all-done = f32[3,8,16,128]{3,2,0,1:T(8,128)S(1)} async-done(((f32[3,8,16,128]{3,2,0,1:T(8,128)}), f32[3,8,16,128]{3,2,0,1:T(8,128)S(1)}, u32[]{:S(2)}, u32[]{:S(2)}) %all-to-all-start) | async-done | bytes 196640 | tf_op jit(solution)/shard_map/all_to_all | solution.py:89
  57.3 3.4 %all-to-all-start.1 = ((f32[3,4,32,128]{3,1,0,2:T(4,128)}), f32[3,4,32,128]{3,1,0,2:T(4,128)S(1)}, u32[]{:S(2)}, u32[]{:S(2)}) async-start(f32[3,4,32,128]{3,1,0,2:T(4,128)} %copy.240), calls=%async_computation.1 | async-start | bytes 393216 | tf_op jit(solution)/shard_map/all_to_all | solution.py:93
  66.4 3.4 %all-to-all-start.2 = ((f32[3,8,16,128]{3,1,0,2:T(8,128)}), f32[3,8,16,128]{3,1,0,2:T(8,128)S(1)}, u32[]{:S(2)}, u32[]{:S(2)}) async-start(f32[3,8,16,128]{3,1,0,2:T(8,128)} %copy.243), calls=%async_computation.2 | async-start | bytes 393216 | tf_op jit(solution)/shard_map/all_to_all | solution.py:96
  71.2 4.5 %collective-permute-start.3 = (f32[8,10,1,128]{3,0,2,1:T(8,128)S(1)}, f32[8,10,1,128]{3,0,2,1:T(8,128)S(1)}, u32[]{:S(2)}, u32[]{:S(2)}) collective-permute-start(f32[8,10,1,128]{3,0,2,1:T(8,128)S(1)} %copy.339), channel_id=1, source_target_pairs={{0,2},{1,3},{4,6},{5,7},{8,10},{9,11},{12,14},{13,15},{16,18},{17,... | collective-permute-start | bytes 122888 | tf_op jit(solution)/shard_map/ppermute | solution.py:24
  78.8 5.0 %all-to-all-start.3 = ((f32[3,32,4,128]{3,2,0,1:T(4,128)}), f32[3,32,4,128]{3,2,0,1:T(4,128)S(1)}, u32[]{:S(2)}, u32[]{:S(2)}) async-start(f32[3,32,4,128]{3,2,0,1:T(4,128)} %copy.247), calls=%async_computation.3 | async-start | bytes 393216 | tf_op jit(solution)/shard_map/all_to_all | solution.py:100
  96.2 3.9 %collective-permute-start.7 = (f32[8,1,16,128]{3,2,1,0:T(8,128)S(1)}, f32[8,1,16,128]{3,2,1,0:T(8,128)S(1)}, u32[]{:S(2)}, u32[]{:S(2)}) collective-permute-start(f32[8,1,16,128]{3,2,1,0:T(8,128)S(1)} %get-tuple-element.53), channel_id=1, source_target_pairs={{0,4},{4,8},{8,12},{1,5},{5,9},{9,13},{2,6},{6,10},{10,14},{3,7},{... | collective-permute-start | bytes 196616 | tf_op jit(solution)/shard_map/ppermute | solution.py:24
  102.0 4.3 %collective-permute-done.6 = f32[8,1,16,128]{3,2,1,0:T(8,128)S(1)} collective-permute-done((f32[8,1,16,128]{3,2,1,0:T(8,128)S(1)}, f32[8,1,16,128]{3,2,1,0:T(8,128)S(1)}, u32[]{:S(2)}, u32[]{:S(2)}) %collective-permute-start.6) | collective-permute-done | bytes 65568 | tf_op jit(solution)/shard_map/ppermute | solution.py:26
  107.7 4.7 %collective-permute-start.9 = (f32[8,10,1,128]{3,0,2,1:T(8,128)S(1)}, f32[8,10,1,128]{3,0,2,1:T(8,128)S(1)}, u32[]{:S(2)}, u32[]{:S(2)}) collective-permute-start(f32[8,10,1,128]{3,0,2,1:T(8,128)S(1)} %copy.341), channel_id=1, source_target_pairs={{0,2},{1,3},{4,6},{5,7},{8,10},{9,11},{12,14},{13,15},{16,18},{17,... | collective-permute-start | bytes 122888 | tf_op jit(solution)/shard_map/ppermute | solution.py:24
  118.1 3.8 %collective-permute-start.11 = (f32[8,10,18,1]{2,0,3,1:T(8,128)S(1)}, f32[8,10,18,1]{2,0,3,1:T(8,128)}, u32[]{:S(2)}, u32[]{:S(2)}) collective-permute-start(f32[8,10,18,1]{2,0,3,1:T(8,128)S(1)} %copy.270), channel_id=1, source_target_pairs={{0,1},{2,3},{4,5},{6,7},{8,9},{10,11},{12,13},{14,15},{16,17},{18,... | collective-permute-start | bytes 17288 | tf_op jit(solution)/shard_map/ppermute | solution.py:24
  128.4 32.9 %all-reduce = (f32[8,3]{0,1:T(4,128)S(1)}, f32[8]{0:T(128)S(1)}, f32[8,3]{0,1:T(4,128)S(1)}) all-reduce(f32[8,3]{0,1:T(4,128)S(1)} %convolution_bitcast_fusion.5, f32[8]{0:T(128)S(1)} %get-tuple-element.10, f32[8,3]{0,1:T(4,128)S(1)} %convolution_bitcast_fusion.4), channel_id=1, replica_groups=mesh['grp'=2,'slab'=4,'row'=2,'col'=2] {'slab','row','col'}, use_global_device_ids=true, to_apply=%region_15.16 | all-reduce | flops 56 | bytes 448 | tf_op jit(solution)/shard_map/psum | solution.py:57
  163.6 2.2 all_gather.7
  166.3 7.4 %all_to_all.144 = f32[3,8,16,128]{3,2,0,1:T(8,128)S(1)} all-to-all(f32[3,8,16,128]{3,2,0,1:T(8,128)S(1)} %fusion.37), channel_id=1, replica_groups=mesh['grp'=2,'slab'=4,'row'=2,'col'=2] {'row'}, dimensions={1} | all-to-all | bytes 393216 | tf_op jit(solution)/shard_map/all_to_all | solution.py:89
  175.0 3.4 %all-to-all-start.5 = ((f32[3,4,32,128]{3,1,0,2:T(4,128)}), f32[3,4,32,128]{3,1,0,2:T(4,128)S(1)}, u32[]{:S(2)}, u32[]{:S(2)}) async-start(f32[3,4,32,128]{3,1,0,2:T(4,128)} %copy.281), calls=%async_computation.5 | async-start | bytes 393216 | tf_op jit(solution)/shard_map/all_to_all | solution.py:93
  184.0 3.4 %all-to-all-start.6 = ((f32[3,8,16,128]{3,1,0,2:T(8,128)}), f32[3,8,16,128]{3,1,0,2:T(8,128)S(1)}, u32[]{:S(2)}, u32[]{:S(2)}) async-start(f32[3,8,16,128]{3,1,0,2:T(8,128)} %copy.284), calls=%async_computation.6 | async-start | bytes 393216 | tf_op jit(solution)/shard_map/all_to_all | solution.py:96
  188.8 4.5 %collective-permute-start.15 = (f32[8,10,1,128]{3,0,2,1:T(8,128)S(1)}, f32[8,10,1,128]{3,0,2,1:T(8,128)S(1)}, u32[]{:S(2)}, u32[]{:S(2)}) collective-permute-start(f32[8,10,1,128]{3,0,2,1:T(8,128)S(1)} %copy.343), channel_id=1, source_target_pairs={{0,2},{1,3},{4,6},{5,7},{8,10},{9,11},{12,14},{13,15},{16,18},{17,... | collective-permute-start | bytes 122888 | tf_op jit(solution)/shard_map/ppermute | solution.py:24
  196.4 5.0 %all-to-all-start.7 = ((f32[3,32,4,128]{3,2,0,1:T(4,128)}), f32[3,32,4,128]{3,2,0,1:T(4,128)S(1)}, u32[]{:S(2)}, u32[]{:S(2)}) async-start(f32[3,32,4,128]{3,2,0,1:T(4,128)} %copy.288), calls=%async_computation.7 | async-start | bytes 393216 | tf_op jit(solution)/shard_map/all_to_all | solution.py:100
  206.3 3.0 %collective-permute-start.17 = (f32[8,10,18,1]{2,0,3,1:T(8,128)S(1)}, f32[8,10,18,1]{2,0,3,1:T(8,128)S(1)}, u32[]{:S(2)}, u32[]{:S(2)}) collective-permute-start(f32[8,10,18,1]{2,0,3,1:T(8,128)S(1)} %copy.303), channel_id=1, source_target_pairs={{0,1},{2,3},{4,5},{6,7},{8,9},{10,11},{12,13},{14,15},{16,17},{18,... | collective-permute-start | bytes 17288 | tf_op jit(solution)/shard_map/ppermute | solution.py:24
  214.0 3.9 %collective-permute-start.19 = (f32[8,1,16,128]{3,2,1,0:T(8,128)S(1)}, f32[8,1,16,128]{3,2,1,0:T(8,128)S(1)}, u32[]{:S(2)}, u32[]{:S(2)}) collective-permute-start(f32[8,1,16,128]{3,2,1,0:T(8,128)S(1)} %get-tuple-element.49), channel_id=1, source_target_pairs={{0,4},{4,8},{8,12},{1,5},{5,9},{9,13},{2,6},{6,10},{10,14},{3,7},{... | collective-permute-start | bytes 196616 | tf_op jit(solution)/shard_map/ppermute | solution.py:24
  219.8 4.3 %collective-permute-done.18 = f32[8,1,16,128]{3,2,1,0:T(8,128)S(1)} collective-permute-done((f32[8,1,16,128]{3,2,1,0:T(8,128)S(1)}, f32[8,1,16,128]{3,2,1,0:T(8,128)S(1)}, u32[]{:S(2)}, u32[]{:S(2)}) %collective-permute-start.18) | collective-permute-done | bytes 65568 | tf_op jit(solution)/shard_map/ppermute | solution.py:26
  225.5 4.8 %collective-permute-start.21 = (f32[8,10,1,128]{3,0,2,1:T(8,128)S(1)}, f32[8,10,1,128]{3,0,2,1:T(8,128)S(1)}, u32[]{:S(2)}, u32[]{:S(2)}) collective-permute-start(f32[8,10,1,128]{3,0,2,1:T(8,128)S(1)} %copy.345), channel_id=1, source_target_pairs={{0,2},{1,3},{4,6},{5,7},{8,10},{9,11},{12,14},{13,15},{16,18},{17,... | collective-permute-start | bytes 122888 | tf_op jit(solution)/shard_map/ppermute | solution.py:24
  234.6 3.0 %collective-permute-start.23 = (f32[8,10,18,1]{2,0,3,1:T(8,128)S(1)}, f32[8,10,18,1]{2,0,3,1:T(8,128)S(1)}, u32[]{:S(2)}, u32[]{:S(2)}) collective-permute-start(f32[8,10,18,1]{2,0,3,1:T(8,128)S(1)} %copy.313), channel_id=1, source_target_pairs={{0,1},{2,3},{4,5},{6,7},{8,9},{10,11},{12,13},{14,15},{16,17},{18,... | collective-permute-start | bytes 17288 | tf_op jit(solution)/shard_map/ppermute | solution.py:24
  (194 shorter events, 81.2 us)
Async XLA Ops:
  47.7 8.5 %all-to-all-start = ((f32[3,8,16,128]{3,2,0,1:T(8,128)}), f32[3,8,16,128]{3,2,0,1:T(8,128)S(1)}, u32[]{:S(2)}, u32[]{:S(2)}) async-start(f32[3,8,16,128]{3,2,0,1:T(8,128)} %fusion.39), calls=%async_computation | async-start | bytes 393216 | tf_op jit(solution)/shard_map/all_to_all | solution.py:89
  57.3 8.2 %all-to-all-start.1 = ((f32[3,4,32,128]{3,1,0,2:T(4,128)}), f32[3,4,32,128]{3,1,0,2:T(4,128)S(1)}, u32[]{:S(2)}, u32[]{:S(2)}) async-start(f32[3,4,32,128]{3,1,0,2:T(4,128)} %copy.240), calls=%async_computation.1 | async-start | bytes 393216 | tf_op jit(solution)/shard_map/all_to_all | solution.py:93
  60.8 8.9 %collective-permute-start.1 = (f32[8,1,16,128]{3,2,1,0:T(8,128)S(1)}, f32[8,1,16,128]{3,2,1,0:T(8,128)S(1)}, u32[]{:S(2)}, u32[]{:S(2)}) collective-permute-start(f32[8,1,16,128]{3,2,1,0:T(8,128)S(1)} %get-tuple-element.55), channel_id=1, source_target_pairs={{0,4},{4,8},{8,12},{1,5},{5,9},{9,13},{2,6},{6,10},{10,14},{3,7},{... | collective-permute-start | bytes 196616 | tf_op jit(solution)/shard_map/ppermute | solution.py:24
  62.1 7.7 %collective-permute-start = (f32[8,1,16,128]{3,2,1,0:T(8,128)S(1)}, f32[8,1,16,128]{3,2,1,0:T(8,128)S(1)}, u32[]{:S(2)}, u32[]{:S(2)}) collective-permute-start(f32[8,1,16,128]{3,2,1,0:T(8,128)S(1)} %get-tuple-element.56), channel_id=1, source_target_pairs={{4,0},{8,4},{12,8},{5,1},{9,5},{13,9},{6,2},{10,6},{14,10},{7,3},{... | collective-permute-start | bytes 196616 | tf_op jit(solution)/shard_map/ppermute | solution.py:26
  66.4 11.2 %all-to-all-start.2 = ((f32[3,8,16,128]{3,1,0,2:T(8,128)}), f32[3,8,16,128]{3,1,0,2:T(8,128)S(1)}, u32[]{:S(2)}, u32[]{:S(2)}) async-start(f32[3,8,16,128]{3,1,0,2:T(8,128)} %copy.243), calls=%async_computation.2 | async-start | bytes 393216 | tf_op jit(solution)/shard_map/all_to_all | solution.py:96
  69.8 5.9 %collective-permute-start.2 = (f32[8,10,1,128]{3,0,2,1:T(8,128)S(1)}, f32[8,10,1,128]{3,0,2,1:T(8,128)S(1)}, u32[]{:S(2)}, u32[]{:S(2)}) collective-permute-start(f32[8,10,1,128]{3,0,2,1:T(8,128)S(1)} %copy.338), channel_id=1, source_target_pairs={{2,0},{3,1},{6,4},{7,5},{10,8},{11,9},{14,12},{15,13},{18,16},{19,... | collective-permute-start | bytes 122888 | tf_op jit(solution)/shard_map/ppermute | solution.py:26
  71.2 6.2 %collective-permute-start.3 = (f32[8,10,1,128]{3,0,2,1:T(8,128)S(1)}, f32[8,10,1,128]{3,0,2,1:T(8,128)S(1)}, u32[]{:S(2)}, u32[]{:S(2)}) collective-permute-start(f32[8,10,1,128]{3,0,2,1:T(8,128)S(1)} %copy.339), channel_id=1, source_target_pairs={{0,2},{1,3},{4,6},{5,7},{8,10},{9,11},{12,14},{13,15},{16,18},{17,... | collective-permute-start | bytes 122888 | tf_op jit(solution)/shard_map/ppermute | solution.py:24
  78.8 15.2 %all-to-all-start.3 = ((f32[3,32,4,128]{3,2,0,1:T(4,128)}), f32[3,32,4,128]{3,2,0,1:T(4,128)S(1)}, u32[]{:S(2)}, u32[]{:S(2)}) async-start(f32[3,32,4,128]{3,2,0,1:T(4,128)} %copy.247), calls=%async_computation.3 | async-start | bytes 393216 | tf_op jit(solution)/shard_map/all_to_all | solution.py:100
  96.2 5.8 %collective-permute-start.7 = (f32[8,1,16,128]{3,2,1,0:T(8,128)S(1)}, f32[8,1,16,128]{3,2,1,0:T(8,128)S(1)}, u32[]{:S(2)}, u32[]{:S(2)}) collective-permute-start(f32[8,1,16,128]{3,2,1,0:T(8,128)S(1)} %get-tuple-element.53), channel_id=1, source_target_pairs={{0,4},{4,8},{8,12},{1,5},{5,9},{9,13},{2,6},{6,10},{10,14},{3,7},{... | collective-permute-start | bytes 196616 | tf_op jit(solution)/shard_map/ppermute | solution.py:24
  100.1 6.2 %collective-permute-start.6 = (f32[8,1,16,128]{3,2,1,0:T(8,128)S(1)}, f32[8,1,16,128]{3,2,1,0:T(8,128)S(1)}, u32[]{:S(2)}, u32[]{:S(2)}) collective-permute-start(f32[8,1,16,128]{3,2,1,0:T(8,128)S(1)} %get-tuple-element.54), channel_id=1, source_target_pairs={{4,0},{8,4},{12,8},{5,1},{9,5},{13,9},{6,2},{10,6},{14,10},{7,3},{... | collective-permute-start | bytes 196616 | tf_op jit(solution)/shard_map/ppermute | solution.py:26
  106.4 6.0 %collective-permute-start.8 = (f32[8,10,1,128]{3,0,2,1:T(8,128)S(1)}, f32[8,10,1,128]{3,0,2,1:T(8,128)S(1)}, u32[]{:S(2)}, u32[]{:S(2)}) collective-permute-start(f32[8,10,1,128]{3,0,2,1:T(8,128)S(1)} %copy.340), channel_id=1, source_target_pairs={{2,0},{3,1},{6,4},{7,5},{10,8},{11,9},{14,12},{15,13},{18,16},{19,... | collective-permute-start | bytes 122888 | tf_op jit(solution)/shard_map/ppermute | solution.py:26
  107.7 6.2 %collective-permute-start.9 = (f32[8,10,1,128]{3,0,2,1:T(8,128)S(1)}, f32[8,10,1,128]{3,0,2,1:T(8,128)S(1)}, u32[]{:S(2)}, u32[]{:S(2)}) collective-permute-start(f32[8,10,1,128]{3,0,2,1:T(8,128)S(1)} %copy.341), channel_id=1, source_target_pairs={{0,2},{1,3},{4,6},{5,7},{8,10},{9,11},{12,14},{13,15},{16,18},{17,... | collective-permute-start | bytes 122888 | tf_op jit(solution)/shard_map/ppermute | solution.py:24
  116.2 5.6 %collective-permute-start.10 = (f32[8,10,18,1]{2,0,3,1:T(8,128)}, f32[8,10,18,1]{2,0,3,1:T(8,128)S(1)}, u32[]{:S(2)}, u32[]{:S(2)}) collective-permute-start(f32[8,10,18,1]{2,0,3,1:T(8,128)} %copy.268), channel_id=1, source_target_pairs={{1,0},{3,2},{5,4},{7,6},{9,8},{11,10},{13,12},{15,14},{17,16},{19,... | collective-permute-start | bytes 17288 | tf_op jit(solution)/shard_map/ppermute | solution.py:26
  175.0 8.2 %all-to-all-start.5 = ((f32[3,4,32,128]{3,1,0,2:T(4,128)}), f32[3,4,32,128]{3,1,0,2:T(4,128)S(1)}, u32[]{:S(2)}, u32[]{:S(2)}) async-start(f32[3,4,32,128]{3,1,0,2:T(4,128)} %copy.281), calls=%async_computation.5 | async-start | bytes 393216 | tf_op jit(solution)/shard_map/all_to_all | solution.py:93
  178.4 8.9 %collective-permute-start.13 = (f32[8,1,16,128]{3,2,1,0:T(8,128)S(1)}, f32[8,1,16,128]{3,2,1,0:T(8,128)S(1)}, u32[]{:S(2)}, u32[]{:S(2)}) collective-permute-start(f32[8,1,16,128]{3,2,1,0:T(8,128)S(1)} %get-tuple-element.51), channel_id=1, source_target_pairs={{0,4},{4,8},{8,12},{1,5},{5,9},{9,13},{2,6},{6,10},{10,14},{3,7},{... | collective-permute-start | bytes 196616 | tf_op jit(solution)/shard_map/ppermute | solution.py:24
  179.7 7.7 %collective-permute-start.12 = (f32[8,1,16,128]{3,2,1,0:T(8,128)S(1)}, f32[8,1,16,128]{3,2,1,0:T(8,128)S(1)}, u32[]{:S(2)}, u32[]{:S(2)}) collective-permute-start(f32[8,1,16,128]{3,2,1,0:T(8,128)S(1)} %get-tuple-element.52), channel_id=1, source_target_pairs={{4,0},{8,4},{12,8},{5,1},{9,5},{13,9},{6,2},{10,6},{14,10},{7,3},{... | collective-permute-start | bytes 196616 | tf_op jit(solution)/shard_map/ppermute | solution.py:26
  184.0 11.2 %all-to-all-start.6 = ((f32[3,8,16,128]{3,1,0,2:T(8,128)}), f32[3,8,16,128]{3,1,0,2:T(8,128)S(1)}, u32[]{:S(2)}, u32[]{:S(2)}) async-start(f32[3,8,16,128]{3,1,0,2:T(8,128)} %copy.284), calls=%async_computation.6 | async-start | bytes 393216 | tf_op jit(solution)/shard_map/all_to_all | solution.py:96
  187.5 5.9 %collective-permute-start.14 = (f32[8,10,1,128]{3,0,2,1:T(8,128)S(1)}, f32[8,10,1,128]{3,0,2,1:T(8,128)S(1)}, u32[]{:S(2)}, u32[]{:S(2)}) collective-permute-start(f32[8,10,1,128]{3,0,2,1:T(8,128)S(1)} %copy.342), channel_id=1, source_target_pairs={{2,0},{3,1},{6,4},{7,5},{10,8},{11,9},{14,12},{15,13},{18,16},{19,... | collective-permute-start | bytes 122888 | tf_op jit(solution)/shard_map/ppermute | solution.py:26
  188.8 6.2 %collective-permute-start.15 = (f32[8,10,1,128]{3,0,2,1:T(8,128)S(1)}, f32[8,10,1,128]{3,0,2,1:T(8,128)S(1)}, u32[]{:S(2)}, u32[]{:S(2)}) collective-permute-start(f32[8,10,1,128]{3,0,2,1:T(8,128)S(1)} %copy.343), channel_id=1, source_target_pairs={{0,2},{1,3},{4,6},{5,7},{8,10},{9,11},{12,14},{13,15},{16,18},{17,... | collective-permute-start | bytes 122888 | tf_op jit(solution)/shard_map/ppermute | solution.py:24
  196.4 15.4 %all-to-all-start.7 = ((f32[3,32,4,128]{3,2,0,1:T(4,128)}), f32[3,32,4,128]{3,2,0,1:T(4,128)S(1)}, u32[]{:S(2)}, u32[]{:S(2)}) async-start(f32[3,32,4,128]{3,2,0,1:T(4,128)} %copy.288), calls=%async_computation.7 | async-start | bytes 393216 | tf_op jit(solution)/shard_map/all_to_all | solution.py:100
  214.0 5.8 %collective-permute-start.19 = (f32[8,1,16,128]{3,2,1,0:T(8,128)S(1)}, f32[8,1,16,128]{3,2,1,0:T(8,128)S(1)}, u32[]{:S(2)}, u32[]{:S(2)}) collective-permute-start(f32[8,1,16,128]{3,2,1,0:T(8,128)S(1)} %get-tuple-element.49), channel_id=1, source_target_pairs={{0,4},{4,8},{8,12},{1,5},{5,9},{9,13},{2,6},{6,10},{10,14},{3,7},{... | collective-permute-start | bytes 196616 | tf_op jit(solution)/shard_map/ppermute | solution.py:24
  217.9 6.2 %collective-permute-start.18 = (f32[8,1,16,128]{3,2,1,0:T(8,128)S(1)}, f32[8,1,16,128]{3,2,1,0:T(8,128)S(1)}, u32[]{:S(2)}, u32[]{:S(2)}) collective-permute-start(f32[8,1,16,128]{3,2,1,0:T(8,128)S(1)} %get-tuple-element.50), channel_id=1, source_target_pairs={{4,0},{8,4},{12,8},{5,1},{9,5},{13,9},{6,2},{10,6},{14,10},{7,3},{... | collective-permute-start | bytes 196616 | tf_op jit(solution)/shard_map/ppermute | solution.py:26
  224.1 6.1 %collective-permute-start.20 = (f32[8,10,1,128]{3,0,2,1:T(8,128)S(1)}, f32[8,10,1,128]{3,0,2,1:T(8,128)S(1)}, u32[]{:S(2)}, u32[]{:S(2)}) collective-permute-start(f32[8,10,1,128]{3,0,2,1:T(8,128)S(1)} %copy.344), channel_id=1, source_target_pairs={{2,0},{3,1},{6,4},{7,5},{10,8},{11,9},{14,12},{15,13},{18,16},{19,... | collective-permute-start | bytes 122888 | tf_op jit(solution)/shard_map/ppermute | solution.py:26
  225.5 6.2 %collective-permute-start.21 = (f32[8,10,1,128]{3,0,2,1:T(8,128)S(1)}, f32[8,10,1,128]{3,0,2,1:T(8,128)S(1)}, u32[]{:S(2)}, u32[]{:S(2)}) collective-permute-start(f32[8,10,1,128]{3,0,2,1:T(8,128)S(1)} %copy.345), channel_id=1, source_target_pairs={{0,2},{1,3},{4,6},{5,7},{8,10},{9,11},{12,14},{13,15},{16,18},{17,... | collective-permute-start | bytes 122888 | tf_op jit(solution)/shard_map/ppermute | solution.py:24
  (26 other events, 231.1 us)
where the time goes:
time: 242 us; the launch traced here: 241 us
  starting transfers between devices  82.7 us (34%)
  blocking collectives  80.2 us (33%)
  waiting for transfers between devices  26.4 us (11%)
  local copies, waits for them, and re-layouts  26 us (11%)
  matrix products  12.9 us (5%)
  other arithmetic  9.53 us (4%)
  between operations  2.89 us (1%)
    psum x2, blocking collectives, class_moments(): lax.psum((jnp.sum(flat, axis=1), jnp.dot(flat, values.T, precision=highes...  68.3 us
    ppermute x12, starting transfers between devices, extended(): lax.ppermute(tail, axis, [(i, (i + 1) % count) for i in range(ends)])  40.1 us
    ppermute x12, starting transfers between devices, extended(): lax.ppermute(head, axis, [((i + 1) % count, i) for i in range(ends)])  15.5 us
    ppermute x12, waiting for transfers between devices, extended(): lax.ppermute(head, axis, [((i + 1) % count, i) for i in range(ends)])  10.2 us
    all_to_all x2, starting transfers between devices, smoothed(): lax.all_to_all(mixed, 'slab', split_axis=1, concat_axis=2, tiled=True)  10.1 us
    slice x8, local copies, waits for them, and re-layouts, extended(): head = lax.slice_in_dim(cells, 0, width, axis=dim)  8.48 us
    all_to_all x1, blocking collectives, smoothed(): lax.all_to_all(across, 'row', split_axis=1, concat_axis=2, tiled=True)  7.42 us
    ppermute x12, waiting for transfers between devices, extended(): lax.ppermute(tail, axis, [(i, (i + 1) % count) for i in range(ends)])  7.35 us
  transfers between devices with their start and end apart: 31, of which 13 were waited for; matrix products, arithmetic and copies ran while one was open for 7% of the time, Pallas kernels for 0%

commit v1 on v0

--- a/solution.py
+++ b/solution.py
@@ -11,6 +11,11 @@
 highest = lax.Precision.HIGHEST
 coupling = 1.0
 breadth = 8.0
+
+
+def axis_by_axis(x, one, other):
+    inner = lax.psum(x, one)
+    return lax.psum(inner, other)
 
 
 def extended(cells, sides, width):
@@ -54,13 +59,14 @@
 def class_moments(belief, corrected):
     flat = belief.reshape(K, -1)
     values = corrected.reshape(M, -1)
-    count, first, squares = lax.psum(
+    count, first, squares = axis_by_axis(
         (
             jnp.sum(flat, axis=1),
             jnp.dot(flat, values.T, precision=highest),
             jnp.dot(flat, (values * values).T, precision=highest),
         ),
-        ("slab", "row", "col"),
+        ("row", "col"),
+        "slab",
     )
     means = first / (count + 1.0)[:, None]
     spread = squares - 2.0 * means * first + means * means * count[:, None]

time: 242 us -> 212 us (0.88)
  blocking collectives: 80.2 us -> 50.2 us
    psum x2 -> x4, blocking collectives: 68.3 us -> 38.3 us  [the longest x2 22.1 us: axis_by_axis(): return lax.psum(inner, other)]
  transfers between devices with their start and end apart: 31 -> 31, of which waited for: 13 -> 13; matrix products, arithmetic and copies ran while one was open for 7% -> 8% of each run, Pallas kernels for 0% -> 0%
where the time goes in v1:
time: 212 us; the launch traced here: 211 us
  starting transfers between devices  83.8 us (40%)
  blocking collectives  50.2 us (24%)
  local copies, waits for them, and re-layouts  26 us (12%)
  waiting for transfers between devices  25.4 us (12%)
  matrix products  12.9 us (6%)
  other arithmetic  9.55 us (5%)
  between operations  2.91 us (1%)
    ppermute x12, starting transfers between devices, extended(): lax.ppermute(tail, axis, [(i, (i + 1) % count) for i in range(ends)])  41.2 us
    psum x2, blocking collectives, axis_by_axis(): return lax.psum(inner, other)  22.1 us
    psum x2, blocking collectives, axis_by_axis(): inner = lax.psum(x, one)  16.3 us
    ppermute x12, starting transfers between devices, extended(): lax.ppermute(head, axis, [((i + 1) % count, i) for i in range(ends)])  15.5 us
    ppermute x12, waiting for transfers between devices, extended(): lax.ppermute(head, axis, [((i + 1) % count, i) for i in range(ends)])  10.2 us
    all_to_all x2, starting transfers between devices, smoothed(): lax.all_to_all(mixed, 'slab', split_axis=1, concat_axis=2, tiled=True)  10.1 us
    slice x8, local copies, waits for them, and re-layouts, extended(): head = lax.slice_in_dim(cells, 0, width, axis=dim)  8.46 us
    all_to_all x1, blocking collectives, smoothed(): lax.all_to_all(across, 'row', split_axis=1, concat_axis=2, tiled=True)  7.42 us
  transfers between devices with their start and end apart: 31, of which 13 were waited for; matrix products, arithmetic and copies ran while one was open for 8% of the time, Pallas kernels for 0%

profile of v1, /device:TPU:0, one launch (start us, length us, event | category | flops | bytes accessed | tf_op | source)
XLA Modules:
  0.0 210.7 jit_solution(15308581820229277952)
XLA Ops:
  6.4 8.5 %all-reduce.1 = (f32[8,3]{0,1:T(4,128)S(1)}, f32[8,3]{0,1:T(4,128)S(1)}, f32[8]{0:T(128)S(1)}) all-reduce(f32[8,3]{0,1:T(4,128)S(1)} %fusion.2, f32[8,3]{0,1:T(4,128)S(1)} %convolution_bitcast_fusion.6, f32[8]{0:T(128)S(1)} %select_reduce_fusion), channel_id=1, replica_groups=mesh['grp'=2,'slab'=4,'row'=2,'col'=2] {'row','col'}, use_global_device_ids=true, to_apply=%region_7.8 | all-reduce | flops 56 | bytes 448 | tf_op jit(solution)/shard_map/psum | solution.py:17
  14.9 12.1 %all-reduce.3 = (f32[8,3]{0,1:T(4,128)S(1)}, f32[8,3]{0,1:T(4,128)S(1)}, f32[8]{0:T(128)S(1)}) all-reduce(f32[8,3]{0,1:T(4,128)S(1)} %get-tuple-element.14, f32[8,3]{0,1:T(4,128)S(1)} %get-tuple-element.15, f32[8]{0:T(128)S(1)} %get-tuple-element.16), channel_id=1, replica_groups=mesh['grp'=2,'slab'=4,'row'=2,'col'=2] {'slab'}, use_global_device_ids=true, to_apply=%region_8.9 | all-reduce | flops 56 | bytes 448 | tf_op jit(solution)/shard_map/psum | solution.py:18
  32.9 3.4 %all-to-all-start = ((f32[3,8,16,128]{3,2,0,1:T(8,128)}), f32[3,8,16,128]{3,2,0,1:T(8,128)S(1)}, u32[]{:S(2)}, u32[]{:S(2)}) async-start(f32[3,8,16,128]{3,2,0,1:T(8,128)} %fusion.39), calls=%async_computation | async-start | bytes 393216 | tf_op jit(solution)/shard_map/all_to_all | solution.py:95
  36.8 4.5 %all-to-all-done = f32[3,8,16,128]{3,2,0,1:T(8,128)S(1)} async-done(((f32[3,8,16,128]{3,2,0,1:T(8,128)}), f32[3,8,16,128]{3,2,0,1:T(8,128)S(1)}, u32[]{:S(2)}, u32[]{:S(2)}) %all-to-all-start) | async-done | bytes 196640 | tf_op jit(solution)/shard_map/all_to_all | solution.py:95
  42.5 3.4 %all-to-all-start.1 = ((f32[3,4,32,128]{3,1,0,2:T(4,128)}), f32[3,4,32,128]{3,1,0,2:T(4,128)S(1)}, u32[]{:S(2)}, u32[]{:S(2)}) async-start(f32[3,4,32,128]{3,1,0,2:T(4,128)} %copy.240), calls=%async_computation.1 | async-start | bytes 393216 | tf_op jit(solution)/shard_map/all_to_all | solution.py:99
  51.6 3.4 %all-to-all-start.2 = ((f32[3,8,16,128]{3,1,0,2:T(8,128)}), f32[3,8,16,128]{3,1,0,2:T(8,128)S(1)}, u32[]{:S(2)}, u32[]{:S(2)}) async-start(f32[3,8,16,128]{3,1,0,2:T(8,128)} %copy.243), calls=%async_computation.2 | async-start | bytes 393216 | tf_op jit(solution)/shard_map/all_to_all | solution.py:102
  56.3 4.5 %collective-permute-start.3 = (f32[8,10,1,128]{3,0,2,1:T(8,128)S(1)}, f32[8,10,1,128]{3,0,2,1:T(8,128)S(1)}, u32[]{:S(2)}, u32[]{:S(2)}) collective-permute-start(f32[8,10,1,128]{3,0,2,1:T(8,128)S(1)} %copy.339), channel_id=1, source_target_pairs={{0,2},{1,3},{4,6},{5,7},{8,10},{9,11},{12,14},{13,15},{16,18},{17,... | collective-permute-start | bytes 122888 | tf_op jit(solution)/shard_map/ppermute | solution.py:29
  64.0 5.0 %all-to-all-start.3 = ((f32[3,32,4,128]{3,2,0,1:T(4,128)}), f32[3,32,4,128]{3,2,0,1:T(4,128)S(1)}, u32[]{:S(2)}, u32[]{:S(2)}) async-start(f32[3,32,4,128]{3,2,0,1:T(4,128)} %copy.247), calls=%async_computation.3 | async-start | bytes 393216 | tf_op jit(solution)/shard_map/all_to_all | solution.py:106
  81.4 3.9 %collective-permute-start.7 = (f32[8,1,16,128]{3,2,1,0:T(8,128)S(1)}, f32[8,1,16,128]{3,2,1,0:T(8,128)S(1)}, u32[]{:S(2)}, u32[]{:S(2)}) collective-permute-start(f32[8,1,16,128]{3,2,1,0:T(8,128)S(1)} %get-tuple-element.59), channel_id=1, source_target_pairs={{0,4},{4,8},{8,12},{1,5},{5,9},{9,13},{2,6},{6,10},{10,14},{3,7},{... | collective-permute-start | bytes 196616 | tf_op jit(solution)/shard_map/ppermute | solution.py:29
  87.2 4.3 %collective-permute-done.6 = f32[8,1,16,128]{3,2,1,0:T(8,128)S(1)} collective-permute-done((f32[8,1,16,128]{3,2,1,0:T(8,128)S(1)}, f32[8,1,16,128]{3,2,1,0:T(8,128)S(1)}, u32[]{:S(2)}, u32[]{:S(2)}) %collective-permute-start.6) | collective-permute-done | bytes 65568 | tf_op jit(solution)/shard_map/ppermute | solution.py:31
  92.9 4.7 %collective-permute-start.9 = (f32[8,10,1,128]{3,0,2,1:T(8,128)S(1)}, f32[8,10,1,128]{3,0,2,1:T(8,128)S(1)}, u32[]{:S(2)}, u32[]{:S(2)}) collective-permute-start(f32[8,10,1,128]{3,0,2,1:T(8,128)S(1)} %copy.341), channel_id=1, source_target_pairs={{0,2},{1,3},{4,6},{5,7},{8,10},{9,11},{12,14},{13,15},{16,18},{17,... | collective-permute-start | bytes 122888 | tf_op jit(solution)/shard_map/ppermute | solution.py:29
  103.3 3.8 %collective-permute-start.11 = (f32[8,10,18,1]{2,0,3,1:T(8,128)S(1)}, f32[8,10,18,1]{2,0,3,1:T(8,128)}, u32[]{:S(2)}, u32[]{:S(2)}) collective-permute-start(f32[8,10,18,1]{2,0,3,1:T(8,128)S(1)} %copy.270), channel_id=1, source_target_pairs={{0,1},{2,3},{4,5},{6,7},{8,9},{10,11},{12,13},{14,15},{16,17},{18,... | collective-permute-start | bytes 17288 | tf_op jit(solution)/shard_map/ppermute | solution.py:29
  113.6 7.8 %all-reduce = (f32[8,3]{0,1:T(4,128)S(1)}, f32[8]{0:T(128)S(1)}, f32[8,3]{0,1:T(4,128)S(1)}) all-reduce(f32[8,3]{0,1:T(4,128)S(1)} %convolution_bitcast_fusion.5, f32[8]{0:T(128)S(1)} %get-tuple-element.10, f32[8,3]{0,1:T(4,128)S(1)} %convolution_bitcast_fusion.4), channel_id=1, replica_groups=mesh['grp'=2,'slab'=4,'row'=2,'col'=2] {'row','col'}, use_global_device_ids=true, to_apply=%region_19.20 | all-reduce | flops 56 | bytes 448 | tf_op jit(solution)/shard_map/psum | solution.py:17
  121.4 10.0 %all-reduce.2 = (f32[8,3]{0,1:T(4,128)S(1)}, f32[8]{0:T(128)S(1)}, f32[8,3]{0,1:T(4,128)S(1)}) all-reduce(f32[8,3]{0,1:T(4,128)S(1)} %get-tuple-element.11, f32[8]{0:T(128)S(1)} %get-tuple-element.12, f32[8,3]{0,1:T(4,128)S(1)} %get-tuple-element.13), channel_id=1, replica_groups=mesh['grp'=2,'slab'=4,'row'=2,'col'=2] {'slab'}, use_global_device_ids=true, to_apply=%region_20.21 | all-reduce | flops 56 | bytes 448 | tf_op jit(solution)/shard_map/psum | solution.py:18
  136.4 7.4 %all_to_all.144 = f32[3,8,16,128]{3,2,0,1:T(8,128)S(1)} all-to-all(f32[3,8,16,128]{3,2,0,1:T(8,128)S(1)} %fusion.37), channel_id=1, replica_groups=mesh['grp'=2,'slab'=4,'row'=2,'col'=2] {'row'}, dimensions={1} | all-to-all | bytes 393216 | tf_op jit(solution)/shard_map/all_to_all | solution.py:95
  145.0 3.4 %all-to-all-start.5 = ((f32[3,4,32,128]{3,1,0,2:T(4,128)}), f32[3,4,32,128]{3,1,0,2:T(4,128)S(1)}, u32[]{:S(2)}, u32[]{:S(2)}) async-start(f32[3,4,32,128]{3,1,0,2:T(4,128)} %copy.281), calls=%async_computation.5 | async-start | bytes 393216 | tf_op jit(solution)/shard_map/all_to_all | solution.py:99
  154.1 3.4 %all-to-all-start.6 = ((f32[3,8,16,128]{3,1,0,2:T(8,128)}), f32[3,8,16,128]{3,1,0,2:T(8,128)S(1)}, u32[]{:S(2)}, u32[]{:S(2)}) async-start(f32[3,8,16,128]{3,1,0,2:T(8,128)} %copy.284), calls=%async_computation.6 | async-start | bytes 393216 | tf_op jit(solution)/shard_map/all_to_all | solution.py:102
  158.8 4.5 %collective-permute-start.15 = (f32[8,10,1,128]{3,0,2,1:T(8,128)S(1)}, f32[8,10,1,128]{3,0,2,1:T(8,128)S(1)}, u32[]{:S(2)}, u32[]{:S(2)}) collective-permute-start(f32[8,10,1,128]{3,0,2,1:T(8,128)S(1)} %copy.343), channel_id=1, source_target_pairs={{0,2},{1,3},{4,6},{5,7},{8,10},{9,11},{12,14},{13,15},{16,18},{17,... | collective-permute-start | bytes 122888 | tf_op jit(solution)/shard_map/ppermute | solution.py:29
  166.5 5.0 %all-to-all-start.7 = ((f32[3,32,4,128]{3,2,0,1:T(4,128)}), f32[3,32,4,128]{3,2,0,1:T(4,128)S(1)}, u32[]{:S(2)}, u32[]{:S(2)}) async-start(f32[3,32,4,128]{3,2,0,1:T(4,128)} %copy.288), calls=%async_computation.7 | async-start | bytes 393216 | tf_op jit(solution)/shard_map/all_to_all | solution.py:106
  176.4 3.0 %collective-permute-start.17 = (f32[8,10,18,1]{2,0,3,1:T(8,128)S(1)}, f32[8,10,18,1]{2,0,3,1:T(8,128)S(1)}, u32[]{:S(2)}, u32[]{:S(2)}) collective-permute-start(f32[8,10,18,1]{2,0,3,1:T(8,128)S(1)} %copy.303), channel_id=1, source_target_pairs={{0,1},{2,3},{4,5},{6,7},{8,9},{10,11},{12,13},{14,15},{16,17},{18,... | collective-permute-start | bytes 17288 | tf_op jit(solution)/shard_map/ppermute | solution.py:29
  184.0 3.9 %collective-permute-start.19 = (f32[8,1,16,128]{3,2,1,0:T(8,128)S(1)}, f32[8,1,16,128]{3,2,1,0:T(8,128)S(1)}, u32[]{:S(2)}, u32[]{:S(2)}) collective-permute-start(f32[8,1,16,128]{3,2,1,0:T(8,128)S(1)} %get-tuple-element.55), channel_id=1, source_target_pairs={{0,4},{4,8},{8,12},{1,5},{5,9},{9,13},{2,6},{6,10},{10,14},{3,7},{... | collective-permute-start | bytes 196616 | tf_op jit(solution)/shard_map/ppermute | solution.py:29
  189.8 4.3 %collective-permute-done.18 = f32[8,1,16,128]{3,2,1,0:T(8,128)S(1)} collective-permute-done((f32[8,1,16,128]{3,2,1,0:T(8,128)S(1)}, f32[8,1,16,128]{3,2,1,0:T(8,128)S(1)}, u32[]{:S(2)}, u32[]{:S(2)}) %collective-permute-start.18) | collective-permute-done | bytes 65568 | tf_op jit(solution)/shard_map/ppermute | solution.py:31
  195.5 4.8 %collective-permute-start.21 = (f32[8,10,1,128]{3,0,2,1:T(8,128)S(1)}, f32[8,10,1,128]{3,0,2,1:T(8,128)S(1)}, u32[]{:S(2)}, u32[]{:S(2)}) collective-permute-start(f32[8,10,1,128]{3,0,2,1:T(8,128)S(1)} %copy.345), channel_id=1, source_target_pairs={{0,2},{1,3},{4,6},{5,7},{8,10},{9,11},{12,14},{13,15},{16,18},{17,... | collective-permute-start | bytes 122888 | tf_op jit(solution)/shard_map/ppermute | solution.py:29
  204.7 3.0 %collective-permute-start.23 = (f32[8,10,18,1]{2,0,3,1:T(8,128)S(1)}, f32[8,10,18,1]{2,0,3,1:T(8,128)S(1)}, u32[]{:S(2)}, u32[]{:S(2)}) collective-permute-start(f32[8,10,18,1]{2,0,3,1:T(8,128)S(1)} %copy.313), channel_id=1, source_target_pairs={{0,1},{2,3},{4,5},{6,7},{8,9},{10,11},{12,13},{14,15},{16,17},{18,... | collective-permute-start | bytes 17288 | tf_op jit(solution)/shard_map/ppermute | solution.py:29
  (196 shorter events, 85.6 us)
Async XLA Ops:
  32.9 8.5 %all-to-all-start = ((f32[3,8,16,128]{3,2,0,1:T(8,128)}), f32[3,8,16,128]{3,2,0,1:T(8,128)S(1)}, u32[]{:S(2)}, u32[]{:S(2)}) async-start(f32[3,8,16,128]{3,2,0,1:T(8,128)} %fusion.39), calls=%async_computation | async-start | bytes 393216 | tf_op jit(solution)/shard_map/all_to_all | solution.py:95
  42.5 8.2 %all-to-all-start.1 = ((f32[3,4,32,128]{3,1,0,2:T(4,128)}), f32[3,4,32,128]{3,1,0,2:T(4,128)S(1)}, u32[]{:S(2)}, u32[]{:S(2)}) async-start(f32[3,4,32,128]{3,1,0,2:T(4,128)} %copy.240), calls=%async_computation.1 | async-start | bytes 393216 | tf_op jit(solution)/shard_map/all_to_all | solution.py:99
  46.0 8.9 %collective-permute-start.1 = (f32[8,1,16,128]{3,2,1,0:T(8,128)S(1)}, f32[8,1,16,128]{3,2,1,0:T(8,128)S(1)}, u32[]{:S(2)}, u32[]{:S(2)}) collective-permute-start(f32[8,1,16,128]{3,2,1,0:T(8,128)S(1)} %get-tuple-element.61), channel_id=1, source_target_pairs={{0,4},{4,8},{8,12},{1,5},{5,9},{9,13},{2,6},{6,10},{10,14},{3,7},{... | collective-permute-start | bytes 196616 | tf_op jit(solution)/shard_map/ppermute | solution.py:29
  47.3 7.7 %collective-permute-start = (f32[8,1,16,128]{3,2,1,0:T(8,128)S(1)}, f32[8,1,16,128]{3,2,1,0:T(8,128)S(1)}, u32[]{:S(2)}, u32[]{:S(2)}) collective-permute-start(f32[8,1,16,128]{3,2,1,0:T(8,128)S(1)} %get-tuple-element.62), channel_id=1, source_target_pairs={{4,0},{8,4},{12,8},{5,1},{9,5},{13,9},{6,2},{10,6},{14,10},{7,3},{... | collective-permute-start | bytes 196616 | tf_op jit(solution)/shard_map/ppermute | solution.py:31
  51.6 11.2 %all-to-all-start.2 = ((f32[3,8,16,128]{3,1,0,2:T(8,128)}), f32[3,8,16,128]{3,1,0,2:T(8,128)S(1)}, u32[]{:S(2)}, u32[]{:S(2)}) async-start(f32[3,8,16,128]{3,1,0,2:T(8,128)} %copy.243), calls=%async_computation.2 | async-start | bytes 393216 | tf_op jit(solution)/shard_map/all_to_all | solution.py:102
  55.0 5.9 %collective-permute-start.2 = (f32[8,10,1,128]{3,0,2,1:T(8,128)S(1)}, f32[8,10,1,128]{3,0,2,1:T(8,128)S(1)}, u32[]{:S(2)}, u32[]{:S(2)}) collective-permute-start(f32[8,10,1,128]{3,0,2,1:T(8,128)S(1)} %copy.338), channel_id=1, source_target_pairs={{2,0},{3,1},{6,4},{7,5},{10,8},{11,9},{14,12},{15,13},{18,16},{19,... | collective-permute-start | bytes 122888 | tf_op jit(solution)/shard_map/ppermute | solution.py:31
  56.3 6.2 %collective-permute-start.3 = (f32[8,10,1,128]{3,0,2,1:T(8,128)S(1)}, f32[8,10,1,128]{3,0,2,1:T(8,128)S(1)}, u32[]{:S(2)}, u32[]{:S(2)}) collective-permute-start(f32[8,10,1,128]{3,0,2,1:T(8,128)S(1)} %copy.339), channel_id=1, source_target_pairs={{0,2},{1,3},{4,6},{5,7},{8,10},{9,11},{12,14},{13,15},{16,18},{17,... | collective-permute-start | bytes 122888 | tf_op jit(solution)/shard_map/ppermute | solution.py:29
  64.0 15.2 %all-to-all-start.3 = ((f32[3,32,4,128]{3,2,0,1:T(4,128)}), f32[3,32,4,128]{3,2,0,1:T(4,128)S(1)}, u32[]{:S(2)}, u32[]{:S(2)}) async-start(f32[3,32,4,128]{3,2,0,1:T(4,128)} %copy.247), calls=%async_computation.3 | async-start | bytes 393216 | tf_op jit(solution)/shard_map/all_to_all | solution.py:106
  81.4 5.8 %collective-permute-start.7 = (f32[8,1,16,128]{3,2,1,0:T(8,128)S(1)}, f32[8,1,16,128]{3,2,1,0:T(8,128)S(1)}, u32[]{:S(2)}, u32[]{:S(2)}) collective-permute-start(f32[8,1,16,128]{3,2,1,0:T(8,128)S(1)} %get-tuple-element.59), channel_id=1, source_target_pairs={{0,4},{4,8},{8,12},{1,5},{5,9},{9,13},{2,6},{6,10},{10,14},{3,7},{... | collective-permute-start | bytes 196616 | tf_op jit(solution)/shard_map/ppermute | solution.py:29
  85.3 6.2 %collective-permute-start.6 = (f32[8,1,16,128]{3,2,1,0:T(8,128)S(1)}, f32[8,1,16,128]{3,2,1,0:T(8,128)S(1)}, u32[]{:S(2)}, u32[]{:S(2)}) collective-permute-start(f32[8,1,16,128]{3,2,1,0:T(8,128)S(1)} %get-tuple-element.60), channel_id=1, source_target_pairs={{4,0},{8,4},{12,8},{5,1},{9,5},{13,9},{6,2},{10,6},{14,10},{7,3},{... | collective-permute-start | bytes 196616 | tf_op jit(solution)/shard_map/ppermute | solution.py:31
  91.5 6.0 %collective-permute-start.8 = (f32[8,10,1,128]{3,0,2,1:T(8,128)S(1)}, f32[8,10,1,128]{3,0,2,1:T(8,128)S(1)}, u32[]{:S(2)}, u32[]{:S(2)}) collective-permute-start(f32[8,10,1,128]{3,0,2,1:T(8,128)S(1)} %copy.340), channel_id=1, source_target_pairs={{2,0},{3,1},{6,4},{7,5},{10,8},{11,9},{14,12},{15,13},{18,16},{19,... | collective-permute-start | bytes 122888 | tf_op jit(solution)/shard_map/ppermute | solution.py:31
  92.9 6.2 %collective-permute-start.9 = (f32[8,10,1,128]{3,0,2,1:T(8,128)S(1)}, f32[8,10,1,128]{3,0,2,1:T(8,128)S(1)}, u32[]{:S(2)}, u32[]{:S(2)}) collective-permute-start(f32[8,10,1,128]{3,0,2,1:T(8,128)S(1)} %copy.341), channel_id=1, source_target_pairs={{0,2},{1,3},{4,6},{5,7},{8,10},{9,11},{12,14},{13,15},{16,18},{17,... | collective-permute-start | bytes 122888 | tf_op jit(solution)/shard_map/ppermute | solution.py:29
  101.4 5.6 %collective-permute-start.10 = (f32[8,10,18,1]{2,0,3,1:T(8,128)}, f32[8,10,18,1]{2,0,3,1:T(8,128)S(1)}, u32[]{:S(2)}, u32[]{:S(2)}) collective-permute-start(f32[8,10,18,1]{2,0,3,1:T(8,128)} %copy.268), channel_id=1, source_target_pairs={{1,0},{3,2},{5,4},{7,6},{9,8},{11,10},{13,12},{15,14},{17,16},{19,... | collective-permute-start | bytes 17288 | tf_op jit(solution)/shard_map/ppermute | solution.py:31
  145.0 8.2 %all-to-all-start.5 = ((f32[3,4,32,128]{3,1,0,2:T(4,128)}), f32[3,4,32,128]{3,1,0,2:T(4,128)S(1)}, u32[]{:S(2)}, u32[]{:S(2)}) async-start(f32[3,4,32,128]{3,1,0,2:T(4,128)} %copy.281), calls=%async_computation.5 | async-start | bytes 393216 | tf_op jit(solution)/shard_map/all_to_all | solution.py:99
  148.5 8.9 %collective-permute-start.13 = (f32[8,1,16,128]{3,2,1,0:T(8,128)S(1)}, f32[8,1,16,128]{3,2,1,0:T(8,128)S(1)}, u32[]{:S(2)}, u32[]{:S(2)}) collective-permute-start(f32[8,1,16,128]{3,2,1,0:T(8,128)S(1)} %get-tuple-element.57), channel_id=1, source_target_pairs={{0,4},{4,8},{8,12},{1,5},{5,9},{9,13},{2,6},{6,10},{10,14},{3,7},{... | collective-permute-start | bytes 196616 | tf_op jit(solution)/shard_map/ppermute | solution.py:29
  150.9 6.6 %collective-permute-start.12 = (f32[8,1,16,128]{3,2,1,0:T(8,128)S(1)}, f32[8,1,16,128]{3,2,1,0:T(8,128)S(1)}, u32[]{:S(2)}, u32[]{:S(2)}) collective-permute-start(f32[8,1,16,128]{3,2,1,0:T(8,128)S(1)} %get-tuple-element.58), channel_id=1, source_target_pairs={{4,0},{8,4},{12,8},{5,1},{9,5},{13,9},{6,2},{10,6},{14,10},{7,3},{... | collective-permute-start | bytes 196616 | tf_op jit(solution)/shard_map/ppermute | solution.py:31
  154.1 11.2 %all-to-all-start.6 = ((f32[3,8,16,128]{3,1,0,2:T(8,128)}), f32[3,8,16,128]{3,1,0,2:T(8,128)S(1)}, u32[]{:S(2)}, u32[]{:S(2)}) async-start(f32[3,8,16,128]{3,1,0,2:T(8,128)} %copy.284), calls=%async_computation.6 | async-start | bytes 393216 | tf_op jit(solution)/shard_map/all_to_all | solution.py:102
  157.5 5.9 %collective-permute-start.14 = (f32[8,10,1,128]{3,0,2,1:T(8,128)S(1)}, f32[8,10,1,128]{3,0,2,1:T(8,128)S(1)}, u32[]{:S(2)}, u32[]{:S(2)}) collective-permute-start(f32[8,10,1,128]{3,0,2,1:T(8,128)S(1)} %copy.342), channel_id=1, source_target_pairs={{2,0},{3,1},{6,4},{7,5},{10,8},{11,9},{14,12},{15,13},{18,16},{19,... | collective-permute-start | bytes 122888 | tf_op jit(solution)/shard_map/ppermute | solution.py:31
  158.8 6.2 %collective-permute-start.15 = (f32[8,10,1,128]{3,0,2,1:T(8,128)S(1)}, f32[8,10,1,128]{3,0,2,1:T(8,128)S(1)}, u32[]{:S(2)}, u32[]{:S(2)}) collective-permute-start(f32[8,10,1,128]{3,0,2,1:T(8,128)S(1)} %copy.343), channel_id=1, source_target_pairs={{0,2},{1,3},{4,6},{5,7},{8,10},{9,11},{12,14},{13,15},{16,18},{17,... | collective-permute-start | bytes 122888 | tf_op jit(solution)/shard_map/ppermute | solution.py:29
  166.5 15.4 %all-to-all-start.7 = ((f32[3,32,4,128]{3,2,0,1:T(4,128)}), f32[3,32,4,128]{3,2,0,1:T(4,128)S(1)}, u32[]{:S(2)}, u32[]{:S(2)}) async-start(f32[3,32,4,128]{3,2,0,1:T(4,128)} %copy.288), calls=%async_computation.7 | async-start | bytes 393216 | tf_op jit(solution)/shard_map/all_to_all | solution.py:106
  184.0 5.8 %collective-permute-start.19 = (f32[8,1,16,128]{3,2,1,0:T(8,128)S(1)}, f32[8,1,16,128]{3,2,1,0:T(8,128)S(1)}, u32[]{:S(2)}, u32[]{:S(2)}) collective-permute-start(f32[8,1,16,128]{3,2,1,0:T(8,128)S(1)} %get-tuple-element.55), channel_id=1, source_target_pairs={{0,4},{4,8},{8,12},{1,5},{5,9},{9,13},{2,6},{6,10},{10,14},{3,7},{... | collective-permute-start | bytes 196616 | tf_op jit(solution)/shard_map/ppermute | solution.py:29
  188.0 6.2 %collective-permute-start.18 = (f32[8,1,16,128]{3,2,1,0:T(8,128)S(1)}, f32[8,1,16,128]{3,2,1,0:T(8,128)S(1)}, u32[]{:S(2)}, u32[]{:S(2)}) collective-permute-start(f32[8,1,16,128]{3,2,1,0:T(8,128)S(1)} %get-tuple-element.56), channel_id=1, source_target_pairs={{4,0},{8,4},{12,8},{5,1},{9,5},{13,9},{6,2},{10,6},{14,10},{7,3},{... | collective-permute-start | bytes 196616 | tf_op jit(solution)/shard_map/ppermute | solution.py:31
  194.2 6.1 %collective-permute-start.20 = (f32[8,10,1,128]{3,0,2,1:T(8,128)S(1)}, f32[8,10,1,128]{3,0,2,1:T(8,128)S(1)}, u32[]{:S(2)}, u32[]{:S(2)}) collective-permute-start(f32[8,10,1,128]{3,0,2,1:T(8,128)S(1)} %copy.344), channel_id=1, source_target_pairs={{2,0},{3,1},{6,4},{7,5},{10,8},{11,9},{14,12},{15,13},{18,16},{19,... | collective-permute-start | bytes 122888 | tf_op jit(solution)/shard_map/ppermute | solution.py:31
  195.5 6.2 %collective-permute-start.21 = (f32[8,10,1,128]{3,0,2,1:T(8,128)S(1)}, f32[8,10,1,128]{3,0,2,1:T(8,128)S(1)}, u32[]{:S(2)}, u32[]{:S(2)}) collective-permute-start(f32[8,10,1,128]{3,0,2,1:T(8,128)S(1)} %copy.345), channel_id=1, source_target_pairs={{0,2},{1,3},{4,6},{5,7},{8,10},{9,11},{12,14},{13,15},{16,18},{17,... | collective-permute-start | bytes 122888 | tf_op jit(solution)/shard_map/ppermute | solution.py:29
  (26 other events, 201.5 us)
